TPU v7x, 32 devices: a whole 2x2x4 slice. The times are simulated.
32 devices in a mesh: rep: 4 (over x, core), dp: 4 (over z), tp: 2 (over y).
Axes of the slice: x: 2, y: 2, z: 4, core: 2. Of those that a mesh axis runs over, the one named last changes fastest.
Arguments:
- hidden: bfloat16 [4, 512, 14336], P('rep', None, 'tp'), may hold values from -6 to 6
- down_weight: bfloat16 [14336, 8192], P('tp', 'dp'), may hold values from -0.046875 to 0.046875
- out_grad: bfloat16 [4, 512, 8192], P('rep', 'tp', 'dp'), may hold values from -6 to 6
- pseudo_grad: bfloat16 [4, 14336, 8192], P('rep', 'tp', 'dp'), may hold values from -6 to 6
- momentum: float32 [14336, 8192], P(('tp', 'rep'), 'dp'), may hold values from -6 to 6
Outputs:
- layer_out: bfloat16 [4, 512, 8192], P('rep', 'tp', 'dp')
- hidden_grad: bfloat16 [4, 512, 14336], P('rep', 'dp', 'tp')
- new_momentum: float32 [14336, 8192], P(('tp', 'rep'), 'dp')
- outer_step: bfloat16 [14336, 8192], P('tp', 'dp')
All inputs are finite; a program needn't handle non-finite values.
Results may differ from a plain program's by a relative error of at most 0.017.
Values may be sent and summed in bfloat16 or wider, within the bound.
No kernel may reach another device: no remote copies, remote signals or barrier semaphores. Data moves between devices by JAX's collectives and lax.ppermute only.
A program may use at most 256 MiB of HBM per device.

v0:
```python
import jax
import jax.numpy as jnp
from jax import lax
from jax.sharding import PartitionSpec as P

outer_rate = 0.7
momentum_rate = 0.9


def per_device(hidden, down_weight, out_grad, pseudo_grad, momentum):
    token_rows = hidden[0]
    local_grads = out_grad[0]
    row_block = token_rows
    layer_out = lax.psum_scatter(
        jnp.dot(row_block, down_weight, preferred_element_type=jnp.float32).astype(jnp.bfloat16),
        "tp",
        scatter_dimension=0,
        tiled=True,
    )
    all_grads = lax.all_gather(local_grads, "tp", axis=0, tiled=True)
    row_block = all_grads
    hidden_grad = lax.psum_scatter(
        lax.dot_general(
            row_block, down_weight, (((1,), (1,)), ((), ())), preferred_element_type=jnp.float32
        ).astype(jnp.bfloat16),
        "dp",
        scatter_dimension=0,
        tiled=True,
    )
    replicas = lax.axis_size("rep")
    replica_terms = pseudo_grad[0].astype(jnp.float32)
    average = (
        lax.psum_scatter(
            replica_terms.astype(jnp.bfloat16), "rep", scatter_dimension=0, tiled=True
        ).astype(jnp.float32)
        / replicas
    )
    new_momentum = momentum_rate * momentum + average
    step_share = (outer_rate * (average + momentum_rate * new_momentum)).astype(jnp.bfloat16)
    outer_step = lax.all_gather(step_share, "rep", axis=0, tiled=True)
    return (layer_out[None], hidden_grad[None], new_momentum, outer_step)


def solution(mesh):
    return jax.shard_map(
        per_device,
        mesh=mesh,
        in_specs=(
            P("rep", None, "tp"),
            P("tp", "dp"),
            P("rep", "tp", "dp"),
            P("rep", "tp", "dp"),
            P(("tp", "rep"), "dp"),
        ),
        out_specs=(
            P("rep", "tp", "dp"),
            P("rep", "dp", "tp"),
            P(("tp", "rep"), "dp"),
            P("tp", "dp"),
        ),
        check_vma=False,
    )
```

profile of v0, /device:TPU:0, one launch (start us, length us, event | category | flops | bytes accessed | tf_op | source)
XLA Modules:
  0.0 610.3 jit_solution(9170276419713844570)
XLA Ops:
  8.0 0.0 reduce-scatter.8.cloned.1.call-start
  8.0 0.7 reduce-scatter.8.cloned.1.call-update
  8.7 0.0 all-gather.6.cloned.1.call-start
  8.8 0.5 all-gather.6.cloned.1.call-update
  9.3 0.0 all-gather.4.cloned.1.call-start
  9.4 214.8 %reduce-scatter.8.cloned.1.call-done = bf16[1792,2048]{1,0:T(8,128)(2,1)} async-done(((bf16[7168,2048]{1,0:T(8,128)(2,1)}), bf16[1792,2048]{1,0:T(8,128)(2,1)}) %reduce-scatter.8.cloned.1.call-update) | async-done | bytes 7340048 | tf_op jit(solution)/shard_map/reduce_scatter | solution.py:33
  224.1 15.4 %multiply_convert_fusion = (bf16[1792,2048]{1,0:T(8,128)(2,1)}, f32[1792,2048]{1,0:T(8,128)}) fusion(bf16[1792,2048]{1,0:T(8,128)(2,1)} %reduce-scatter.8.cloned.1.call-done, f32[1792,2048]{1,0:T(8,128)} %param.9), kind=kLoop, calls=%fused_computation | loop fusion | flops 29360128 | bytes 44040192 | tf_op jit(solution)/shard_map/convert_element_type | solution.py:39
  239.5 0.0 all-gather.4.cloned.1.call-update
  239.5 0.0 reduce-scatter.4.cloned.1.call-start
  239.6 24.8 %fusion.3 = bf16[512,2048]{1,0:T(8,128)(2,1)} fusion(bf16[7168,2048]{1,0:T(8,128)(2,1)} %param.6, bf16[1,512,7168]{2,1,0:T(8,128)(2,1)} %param.5), kind=kOutput, calls=%fused_computation.6 | convolution fusion | flops 15033434112 | bytes 38797312 | tf_op jit(solution)/shard_map/dot_general | solution.py:15
  264.4 0.0 reduce-scatter.4.cloned.1.call-update
  264.4 0.0 reduce-scatter.6.cloned.1.call-start
  264.5 0.0 all-gather.6.cloned.1.call-done
  264.5 23.1 %convolution_convert_fusion = bf16[512,7168]{1,0:T(8,128)(2,1)} fusion(bf16[7168,2048]{1,0:T(8,128)(2,1)} %param.6, bf16[1,512,2048]{2,1,0:T(8,128)(2,1)} %all-gather.6.cloned.1.call-done), kind=kOutput, calls=%fused_computation.3 | convolution fusion | flops 15036055552 | bytes 38797312 | tf_op jit(solution)/shard_map/dot_general | solution.py:23
  287.6 0.0 reduce-scatter.6.cloned.1.call-update
  287.6 129.9 %all-gather.4.cloned.1.call-done = bf16[7168,2048]{1,0:T(8,128)(2,1)} async-done(((bf16[1792,2048]{1,0:T(8,128)(2,1)}), bf16[7168,2048]{1,0:T(8,128)(2,1)}) %all-gather.4.cloned.1.call-update) | async-done | bytes 29360144 | tf_op jit(solution)/shard_map/all_gather | solution.py:40
  417.5 34.5 %reduce-scatter.4.cloned.1.call-done = bf16[256,2048]{1,0:T(8,128)(2,1)} async-done(((bf16[512,2048]{1,0:T(8,128)(2,1)}), bf16[256,2048]{1,0:T(8,128)(2,1)}) %reduce-scatter.4.cloned.1.call-update) | async-done | bytes 1048592 | tf_op jit(solution)/shard_map/reduce_scatter | solution.py:14
  452.0 130.6 %reduce-scatter.6.cloned.1.call-done = bf16[128,7168]{1,0:T(8,128)(2,1)} async-done(((bf16[512,7168]{1,0:T(8,128)(2,1)}), bf16[128,7168]{1,0:T(8,128)(2,1)}) %reduce-scatter.6.cloned.1.call-update) | async-done | bytes 1835024 | tf_op jit(solution)/shard_map/reduce_scatter | solution.py:22
  582.7 20.1 %copy.10 = bf16[7168,2048]{1,0:T(8,128)(2,1)} copy(bf16[7168,2048]{1,0:T(8,128)(2,1)} %all-gather.4.cloned.1.call-done) | data formatting | bytes 58720256
Async XLA Ops:
  8.0 216.1 %reduce-scatter.8.cloned.1.call-start = ((), (), s32[]{:S(2)}) async-start(), calls=%async_computation.5 | async-start | bytes 36700160 | tf_op jit(solution)/shard_map/reduce_scatter | solution.py:33
  8.7 255.8 %all-gather.6.cloned.1.call-start = ((), (), s32[]{:S(2)}) async-start(), calls=%async_computation.7 | async-start | bytes 3145728 | tf_op jit(solution)/shard_map/all_gather | solution.py:20
  9.3 408.2 %all-gather.4.cloned.1.call-start = ((), (), s32[]{:S(2)}) async-start(), calls=%async_computation.6 | async-start | bytes 36700160 | tf_op jit(solution)/shard_map/all_gather | solution.py:40
  239.5 212.5 %reduce-scatter.4.cloned.1.call-start = ((), (), s32[]{:S(2)}) async-start(), calls=%async_computation.3 | async-start | bytes 3145728 | tf_op jit(solution)/shard_map/reduce_scatter | solution.py:14
  264.4 318.3 %reduce-scatter.6.cloned.1.call-start = ((), (), s32[]{:S(2)}) async-start(), calls=%async_computation.4 | async-start | bytes 9175040 | tf_op jit(solution)/shard_map/reduce_scatter | solution.py:22
Sparse Core Ops, SparseCore 0:
  11.4 212.6 reduce-scatter.7
Sparse Core Ops, SparseCore 1:
  10.8 35.7 all-gather.5
  239.6 177.8 all-gather.3
  420.2 31.8 reduce-scatter.3
  454.9 127.7 reduce-scatter.5
where the time goes:
time: 610 us
  waiting for transfers between devices  511 us (84%)
  matrix products  47.9 us (8%)
  local copies, waits for them, and re-layouts  20.1 us (3%)
  between operations  15.7 us (3%)
  other arithmetic  15.4 us (3%)
    reduce_scatter x1, waiting for transfers between devices, per_device(): lax.psum_scatter(replica_terms.astype(jnp.bfloat16), 'rep', scatter_dimen...  215 us
    reduce_scatter x1, waiting for transfers between devices, per_device(): lax.psum_scatter(lax.dot_general(row_block, down_weight, (((1,), (1,)), (...  131 us
    all_gather x1, waiting for transfers between devices, per_device(): outer_step = lax.all_gather(step_share, 'rep', axis=0, tiled=True)  130 us
    reduce_scatter x1, waiting for transfers between devices, per_device(): lax.psum_scatter(jnp.dot(row_block, down_weight, preferred_element_type=j...  34.5 us
    dot_general x1, matrix products, per_device(): jnp.dot(row_block, down_weight, preferred_element_type=jnp.float32)  24.8 us
    dot_general x1, matrix products, per_device(): lax.dot_general(row_block, down_weight, (((1,), (1,)), ((), ())), preferr...  23.1 us
    unnamed x1, local copies, waits for them, and re-layouts  20.1 us
    convert_element_type x1, other arithmetic, per_device(): (outer_rate * (average + momentum_rate * new_momentum)).astype(jnp.bfloat16)  15.4 us
  transfers between devices with their start and end apart: 5, of which 4 were waited for; matrix products, arithmetic and copies ran while one was open for 10% of the time, Pallas kernels for 0%

commit v1 on v0

v1 whole, which is shorter than its diff:
```python
import jax
import jax.numpy as jnp
from jax import lax
from jax.sharding import PartitionSpec as P


outer_rate = 0.7
momentum_rate = 0.9
piece_units = (1, 3, 5, 4, 1)


def piece_sizes(rows, tile=16):
    if rows % (sum(piece_units) * tile) == 0:
        return [rows // sum(piece_units) * u for u in piece_units]
    return [rows]


def after(index, value):
    return lax.optimization_barrier((index, value))[0]


def outer_update(pseudo, momentum):
    replicas = lax.axis_size("rep")
    lanes = 2 if replicas % 2 == 0 else 1
    groups = replicas // lanes
    me = lax.axis_index("rep")
    lane, group = me % lanes, me // lanes
    mate_perm = [(r, r ^ 1) for r in range(replicas)]
    rows, width = momentum.shape
    sizes = piece_sizes(rows)
    starts = [sum(sizes[:j]) for j in range(len(sizes))]
    pieces = range(len(sizes))
    shifts = range(1, groups)

    def to_mate(value):
        return lax.ppermute(value, "rep", mate_perm)

    def to_group(value, shift):
        perm = [(r, (r // lanes + shift) % groups * lanes + r % lanes) for r in range(replicas)]
        return lax.ppermute(value, "rep", perm)

    def block_of(shift, mate):
        owner = (group + shift) % groups * lanes + (lanes - 1 - lane if mate else lane)
        return owner * rows

    def chip_sum(shift, j, last):
        mine, theirs = block_of(shift, False) + starts[j], block_of(shift, True) + starts[j]
        if last is not None:
            mine, theirs = after((mine, theirs), last)
        total = lax.dynamic_slice(pseudo, (mine, 0), (sizes[j], width)).astype(jnp.float32)
        if lanes == 2:
            other = to_mate(lax.dynamic_slice(pseudo, (theirs, 0), (sizes[j], width)))
            total = total + other.astype(jnp.float32)
        return total

    last = None
    incoming = [[] for _ in pieces]
    for j in pieces:
        for s in shifts:
            value = chip_sum(s, j, last).astype(jnp.bfloat16)
            incoming[j].append(to_group(value, s))
            last = value
    sent = last
    new_momentum = jnp.zeros_like(momentum)
    outer_step = jnp.zeros_like(pseudo)
    own_mine, own_theirs = block_of(0, False), block_of(0, True)
    if sent is not None:
        own_mine, own_theirs = after((own_mine, own_theirs), sent)
    own = None
    if lanes == 2:
        own = to_mate(lax.dynamic_slice(pseudo, (own_theirs, 0), (rows, width)))
    returned = []
    for j in pieces:
        total = lax.dynamic_slice(pseudo, (own_mine + starts[j], 0), (sizes[j], width))
        total = total.astype(jnp.float32)
        if own is not None:
            total = total + lax.slice_in_dim(own, starts[j], starts[j] + sizes[j]).astype(
                jnp.float32
            )
        for piece in incoming[j]:
            total = total + piece.astype(jnp.float32)
        average = total / replicas
        old = lax.slice_in_dim(momentum, starts[j], starts[j] + sizes[j], axis=0)
        fresh = momentum_rate * old + average
        share = (outer_rate * (average + momentum_rate * fresh)).astype(jnp.bfloat16)
        new_momentum = lax.dynamic_update_slice(new_momentum, fresh, (starts[j], 0))
        returned.append([(s, to_group(share, s)) for s in shifts])
        outer_step = lax.dynamic_update_slice(
            outer_step, share, (block_of(0, False) + starts[j], 0)
        )
        if lanes == 2:
            outer_step = lax.dynamic_update_slice(
                outer_step, to_mate(share), (block_of(0, True) + starts[j], 0)
            )
    for j in pieces:
        for s, mine in returned[j]:
            outer_step = lax.dynamic_update_slice(
                outer_step, mine, (block_of(-s, False) + starts[j], 0)
            )
            if lanes == 2:
                outer_step = lax.dynamic_update_slice(
                    outer_step, to_mate(mine), (block_of(-s, True) + starts[j], 0)
                )
    return new_momentum, outer_step, sent


def per_device(hidden, down_weight, out_grad, pseudo_grad, momentum):
    new_momentum, outer_step, _ = outer_update(pseudo_grad[0], momentum)
    partial_out = jnp.dot(hidden[0], down_weight, preferred_element_type=jnp.float32)
    layer_out = lax.psum_scatter(
        partial_out.astype(jnp.bfloat16), "tp", scatter_dimension=0, tiled=True
    )
    all_grads = lax.all_gather(out_grad[0], "tp", axis=0, tiled=True)
    partial_back = lax.dot_general(
        all_grads, down_weight, (((1,), (1,)), ((), ())), preferred_element_type=jnp.float32
    )
    hidden_grad = lax.psum_scatter(
        partial_back.astype(jnp.bfloat16), "dp", scatter_dimension=0, tiled=True
    )
    return (layer_out[None], hidden_grad[None], new_momentum, outer_step)


def solution(mesh):
    return jax.shard_map(
        per_device,
        mesh=mesh,
        in_specs=(
            P("rep", None, "tp"),
            P("tp", "dp"),
            P("rep", "tp", "dp"),
            P("rep", "tp", "dp"),
            P(("tp", "rep"), "dp"),
        ),
        out_specs=(
            P("rep", "tp", "dp"),
            P("rep", "dp", "tp"),
            P(("tp", "rep"), "dp"),
            P("tp", "dp"),
        ),
        check_vma=False,
    )
```

time: 610 us -> 444 us (0.73)
  waiting for transfers between devices: 511 us -> 234 us
  local copies, waits for them, and re-layouts: 20.1 us -> 68.7 us
  other arithmetic: 15.4 us -> 62.1 us
  starting transfers between devices: 0.21 us -> 18 us
    reduce_scatter x3 -> x2, waiting for transfers between devices: 380 us -> 0.01 us  [the longest x1 0.01 us: per_device(): lax.psum_scatter(partial_out.astype(jnp.bfloat16), 'tp', scatter_dimensio...]
    ppermute x0 -> x26, waiting for transfers between devices: none -> 234 us  [the longest x10 216 us: to_group(): return lax.ppermute(value, 'rep', perm)]
    all_gather x2 -> x1, waiting for transfers between devices: 130 us -> 0.01 us  [per_device(): all_grads = lax.all_gather(out_grad[0], 'tp', axis=0, tiled=True)]
    dynamic_update_slice x0 -> x9, other arithmetic: none -> 46.6 us  [the longest x5 25.3 us: outer_update(): lax.dynamic_update_slice(outer_step, share, (block_of(0, False) + starts[...]
    dynamic_update_slice x0 -> x16, local copies, waits for them, and re-layouts: none -> 38.4 us  [the longest x5 12.3 us: outer_update(): lax.dynamic_update_slice(outer_step, to_mate(share), (block_of(0, True) +...]
    dynamic_slice x0 -> x6, local copies, waits for them, and re-layouts: none -> 20.4 us  [the longest x5 11.6 us: chip_sum(): other = to_mate(lax.dynamic_slice(pseudo, (theirs, 0), (sizes[j], width)))]
    unnamed x1 -> x12, local copies, waits for them, and re-layouts: 20.1 us -> 0.02 us
    ppermute x0 -> x26, starting transfers between devices: none -> 17.4 us  [the longest x10 14 us: to_group(): return lax.ppermute(value, 'rep', perm)]
  transfers between devices with their start and end apart: 5 -> 29, of which waited for: 4 -> 13; matrix products, arithmetic and copies ran while one was open for 10% -> 34% of each run, Pallas kernels for 0% -> 0%
where the time goes in v1:
time: 444 us
  waiting for transfers between devices  234 us (53%)
  local copies, waits for them, and re-layouts  68.7 us (15%)
  other arithmetic  62.1 us (14%)
  matrix products  46.4 us (10%)
  starting transfers between devices  18 us (4%)
  between operations  14 us (3%)
    ppermute x10, waiting for transfers between devices, to_group(): return lax.ppermute(value, 'rep', perm)  216 us
    dynamic_update_slice x5, other arithmetic, outer_update(): lax.dynamic_update_slice(outer_step, share, (block_of(0, False) + starts[...  25.3 us
    dot_general x1, matrix products, per_device(): jnp.dot(hidden[0], down_weight, preferred_element_type=jnp.float32)  23.7 us
    dot_general x1, matrix products, per_device(): lax.dot_general(all_grads, down_weight, (((1,), (1,)), ((), ())), preferr...  22.7 us
    dynamic_update_slice x4, other arithmetic, outer_update(): new_momentum = lax.dynamic_update_slice(new_momentum, fresh, (starts[j], 0))  21.4 us
    ppermute x16, waiting for transfers between devices, to_mate(): return lax.ppermute(value, 'rep', mate_perm)  18.4 us
    convert_element_type x5, other arithmetic, outer_update(): value = chip_sum(s, j, last).astype(jnp.bfloat16)  15.5 us
    ppermute x10, starting transfers between devices, to_group(): return lax.ppermute(value, 'rep', perm)  14 us
  transfers between devices with their start and end apart: 29, of which 13 were waited for; matrix products, arithmetic and copies ran while one was open for 34% of the time, Pallas kernels for 0%

profile of v1, /device:TPU:0, one launch (start us, length us, event | category | flops | bytes accessed | tf_op | source)
XLA Modules:
  0.0 443.5 jit_solution(6842654326908805330)
XLA Ops:
  14.6 3.0 collective-permute-done.1
  17.7 3.2 fusion.12
  20.9 4.0 dynamic-slice_bitcast_fusion.1
  25.3 4.7 %collective-permute-done.2 = bf16[640,2048]{1,0:T(8,128)(2,1)S(1)} collective-permute-done((bf16[640,2048]{1,0:T(8,128)(2,1)}, bf16[640,2048]{1,0:T(8,128)(2,1)S(1)}, u32[]{:S(2)}, u32[]{:S(2)}) %collective-permute-start.2) | collective-permute-done | bytes 2621472 | tf_op jit(solution)/shard_map/ppermute | solution.py:36
  30.0 4.5 %fusion.4 = bf16[640,2048]{1,0:T(8,128)(2,1)} fusion(bf16[640,2048]{1,0:T(8,128)(2,1)S(1)} %collective-permute-done.2, bf16[1,7168,2048]{2,1,0:T(8,128)(2,1)} %param.8, s32[]{:T(128)S(6)} %select_n.197), kind=kLoop, calls=%fused_computation.8 | loop fusion | flops 5242880 | bytes 7864324 | tf_op jit(solution)/shard_map/convert_element_type | solution.py:60
  34.5 3.5 dynamic-slice_bitcast_fusion.2
  38.4 4.0 collective-permute-done.3
  42.4 3.8 fusion.8
  51.4 8.8 %dynamic-slice_bitcast_fusion = bf16[1792,2048]{1,0:T(8,128)(2,1)} fusion(bf16[1,7168,2048]{2,1,0:T(8,128)(2,1)} %param.8, s32[]{:T(128)S(6)} %select_n.204), kind=kLoop, calls=%fused_computation.3 | loop fusion | bytes 14680068 | tf_op jit(solution)/shard_map/dynamic_slice | solution.py:71
  60.6 23.7 %fusion.13 = bf16[512,2048]{1,0:T(8,128)(2,1)} fusion(bf16[7168,2048]{1,0:T(8,128)(2,1)} %param.6, bf16[1,512,7168]{2,1,0:T(8,128)(2,1)} %param.5), kind=kOutput, calls=%fused_computation.27 | convolution fusion | flops 15033434112 | bytes 38797312 | tf_op jit(solution)/shard_map/dot_general | solution.py:109
  87.4 22.7 %convolution_convert_fusion = bf16[512,7168]{1,0:T(8,128)(2,1)} fusion(bf16[7168,2048]{1,0:T(8,128)(2,1)} %param.6, bf16[1,512,2048]{2,1,0:T(8,128)(2,1)} %all-gather.3.cloned.1.call-done), kind=kOutput, calls=%fused_computation | convolution fusion | flops 15036055552 | bytes 38797312 | tf_op jit(solution)/shard_map/dot_general | solution.py:114
  110.2 9.9 %broadcast_in_dim.12 = bf16[7168,2048]{1,0:T(8,128)(2,1)} broadcast(bf16[]{:T(256)} %constant.176.clone.1), dimensions={} | broadcast | bytes 29360130 | tf_op jit(solution)/shard_map/broadcast_in_dim | solution.py:65
  120.1 3.2 constant_dynamic-update-slice_fusion.19
  127.2 6.7 %collective-permute-done.7 = bf16[384,2048]{1,0:T(8,128)(2,1)} collective-permute-done((bf16[384,2048]{1,0:T(8,128)(2,1)}, bf16[384,2048]{1,0:T(8,128)(2,1)}, u32[]{:S(2)}, u32[]{:S(2)}) %collective-permute-start.7) | collective-permute-done | bytes 1572896 | tf_op jit(solution)/shard_map/ppermute | solution.py:40
  133.9 6.6 %constant_dynamic-update-slice_fusion.17 = (bf16[7168,2048]{1,0:T(8,128)(2,1)}, bf16[384,2048]{1,0:T(8,128)(2,1)}) fusion(bf16[7168,2048]{1,0:T(8,128)(2,1)} %constant_dynamic-update-slice_fusion.18, s32[]{:T(128)S(6)} %select_n.211, f32[1792,2048]{1,0:T(8,128)} %param.9, bf16[384,2048]{1,0:T(8,128)(2,1)} %collective-permute-done.7, ...), kind=kLoop, calls=%fused_computation.67 | loop fusion | flops 9437184 | bytes 11010056 | tf_op jit(solution)/shard_map/dynamic_update_slice | solution.py:88
  140.5 3.7 collective-permute-done.12
  144.2 2.7 constant_dynamic-update-slice_fusion.16
  147.0 42.7 %collective-permute-done.8 = bf16[640,2048]{1,0:T(8,128)(2,1)S(1)} collective-permute-done((bf16[640,2048]{1,0:T(8,128)(2,1)}, bf16[640,2048]{1,0:T(8,128)(2,1)S(1)}, u32[]{:S(2)}, u32[]{:S(2)}) %collective-permute-start.8) | collective-permute-done | bytes 2621472 | tf_op jit(solution)/shard_map/ppermute | solution.py:40
  189.6 6.7 %constant_dynamic-update-slice_fusion.15 = (bf16[7168,2048]{1,0:T(8,128)(2,1)}, bf16[640,2048]{1,0:T(8,128)(2,1)}) fusion(bf16[7168,2048]{1,0:T(8,128)(2,1)} %constant_dynamic-update-slice_fusion.16, s32[]{:T(128)S(6)} %select_n.213, f32[1792,2048]{1,0:T(8,128)} %param.9, bf16[640,2048]{1,0:T(8,128)(2,1)S(1)} %collective-permute-done.8, ...), kind=kLoop, calls=%fused_computation.65 | loop fusion | flops 15728640 | bytes 18350088 | tf_op jit(solution)/shard_map/dynamic_update_slice | solution.py:88
  198.4 8.7 %dynamic_update_slice.75 = f32[1792,2048]{1,0:T(8,128)} pad(f32[128,2048]{1,0:T(8,128)} %get-tuple-element.34, f32[]{:T(128)} %constant.171.clone.1), padding=0_1664x0_0 | pad | bytes 15728644 | tf_op jit(solution)/shard_map/dynamic_update_slice | solution.py:86
  208.8 3.7 constant_dynamic-update-slice_fusion.14
  212.6 32.6 %collective-permute-done.9 = bf16[512,2048]{1,0:T(8,128)(2,1)} collective-permute-done((bf16[512,2048]{1,0:T(8,128)(2,1)}, bf16[512,2048]{1,0:T(8,128)(2,1)}, u32[]{:S(2)}, u32[]{:S(2)}) %collective-permute-start.9) | collective-permute-done | bytes 2097184 | tf_op jit(solution)/shard_map/ppermute | solution.py:40
  245.2 6.3 %constant_dynamic-update-slice_fusion.13 = (bf16[7168,2048]{1,0:T(8,128)(2,1)}, bf16[512,2048]{1,0:T(8,128)(2,1)}) fusion(bf16[7168,2048]{1,0:T(8,128)(2,1)} %constant_dynamic-update-slice_fusion.14, s32[]{:T(128)S(6)} %select_n.215, f32[1792,2048]{1,0:T(8,128)} %param.9, bf16[512,2048]{1,0:T(8,128)(2,1)} %collective-permute-done.9, ...), kind=kLoop, calls=%fused_computation.63 | loop fusion | flops 12582912 | bytes 14680072 | tf_op jit(solution)/shard_map/dynamic_update_slice | solution.py:88
  251.6 5.2 %fusion.16 = f32[1792,2048]{1,0:T(8,128)} fusion(f32[1792,2048]{1,0:T(8,128)} %dynamic_update_slice.75, f32[1792,2048]{1,0:T(8,128)S(1)} %bitcast.66, bf16[384,2048]{1,0:T(8,128)(2,1)} %collective-permute-done.7, bf16[1792,2048]{1,0:T(8,128)(2,1)} %collective-permute-done.5, bf16[1,7168,2048]{2,1,0:T(8,128)(2,1)} %param.8, s32[]{:T(128)S(6)} %select_n.205), kind=kLoop, calls=%fused_computation.29 | loop fusion | flops 6291456 | bytes 11010052 | tf_op jit(solution)/shard_map/dynamic_update_slice | solution.py:86
  258.8 7.0 %fusion.5 = f32[1792,2048]{1,0:T(8,128)} fusion(f32[1792,2048]{1,0:T(8,128)} %fusion.16, f32[1792,2048]{1,0:T(8,128)S(1)} %bitcast.66, bf16[640,2048]{1,0:T(8,128)(2,1)S(1)} %collective-permute-done.8, bf16[1792,2048]{1,0:T(8,128)(2,1)} %collective-permute-done.5, bf16[1,7168,2048]{2,1,0:T(8,128)(2,1)} %param.8, s32[]{:T(128)S(6)} %select_n.206), kind=kLoop, calls=%fused_computation.11 | loop fusion | flops 10485760 | bytes 18350084 | tf_op jit(solution)/shard_map/dynamic_update_slice | solution.py:86
  267.6 6.5 %fusion.9 = f32[1792,2048]{1,0:T(8,128)} fusion(f32[1792,2048]{1,0:T(8,128)} %fusion.5, f32[1792,2048]{1,0:T(8,128)S(1)} %bitcast.66, bf16[512,2048]{1,0:T(8,128)(2,1)} %collective-permute-done.9, bf16[1792,2048]{1,0:T(8,128)(2,1)} %collective-permute-done.5, bf16[1,7168,2048]{2,1,0:T(8,128)(2,1)} %param.8, s32[]{:T(128)S(6)} %select_n.207), kind=kLoop, calls=%fused_computation.19 | loop fusion | flops 8388608 | bytes 14680068 | tf_op jit(solution)/shard_map/dynamic_update_slice | solution.py:86
  274.2 72.1 %collective-permute-done.18 = bf16[384,2048]{1,0:T(8,128)(2,1)} collective-permute-done((bf16[384,2048]{1,0:T(8,128)(2,1)}, bf16[384,2048]{1,0:T(8,128)(2,1)}, u32[]{:S(2)}, u32[]{:S(2)}) %collective-permute-start.18) | collective-permute-done | bytes 1572896 | tf_op jit(solution)/shard_map/ppermute | solution.py:40
  346.9 3.2 constant_dynamic-update-slice_fusion.12
  350.1 51.9 %collective-permute-done.10 = bf16[128,2048]{1,0:T(8,128)(2,1)S(1)} collective-permute-done((bf16[128,2048]{1,0:T(8,128)(2,1)S(1)}, bf16[128,2048]{1,0:T(8,128)(2,1)S(1)}, u32[]{:S(2)}, u32[]{:S(2)}) %collective-permute-start.10) | collective-permute-done | bytes 524320 | tf_op jit(solution)/shard_map/ppermute | solution.py:40
  408.9 9.8 %collective-permute-done.24 = bf16[128,2048]{1,0:T(8,128)(2,1)S(1)} collective-permute-done((bf16[128,2048]{1,0:T(8,128)(2,1)S(1)}, bf16[128,2048]{1,0:T(8,128)(2,1)S(1)}, u32[]{:S(2)}, u32[]{:S(2)}) %collective-permute-start.24) | collective-permute-done | bytes 524320 | tf_op jit(solution)/shard_map/ppermute | solution.py:40
  425.2 3.6 constant_dynamic-update-slice_fusion.5
  430.6 3.2 constant_dynamic-update-slice_fusion.3
  (81 shorter events, 47.4 us)
Async XLA Ops:
  7.2 80.3 %all-gather.3.cloned.1.call-start = ((), (), s32[]{:S(2)}) async-start(), calls=%async_computation.4 | async-start | bytes 3145728 | tf_op jit(solution)/shard_map/all_gather | solution.py:113
  8.3 2.1 collective-permute-start
  14.2 3.5 collective-permute-start.1
  24.9 5.1 %collective-permute-start.2 = (bf16[640,2048]{1,0:T(8,128)(2,1)}, bf16[640,2048]{1,0:T(8,128)(2,1)S(1)}, u32[]{:S(2)}, u32[]{:S(2)}) collective-permute-start(bf16[640,2048]{1,0:T(8,128)(2,1)} %dynamic-slice_bitcast_fusion.1), channel_id=1, source_target_pairs={{0,8},{8,0},{16,24},{24,16},{1,9},{9,1},{17,25},{25,17},{2,10},{10... | collective-permute-start | bytes 7864328 | tf_op jit(solution)/shard_map/ppermute | solution.py:36
  38.0 4.4 collective-permute-start.3
  47.3 2.0 collective-permute-start.4
  47.8 389.2 %reduce-scatter.3.cloned.1.call-start = ((), (), s32[]{:S(2)}) async-start(), calls=%async_computation.2 | async-start | bytes 3145728 | tf_op jit(solution)/shard_map/reduce_scatter | solution.py:110
  60.2 50.0 %collective-permute-start.5 = (bf16[1792,2048]{1,0:T(8,128)(2,1)}, bf16[1792,2048]{1,0:T(8,128)(2,1)}, u32[]{:S(2)}, u32[]{:S(2)}) collective-permute-start(bf16[1792,2048]{1,0:T(8,128)(2,1)} %dynamic-slice_bitcast_fusion), channel_id=1, source_target_pairs={{0,8},{8,0},{16,24},{24,16},{1,9},{9,1},{17,25},{25,17},{2,10},{10... | collective-permute-start | bytes 22020104 | tf_op jit(solution)/shard_map/ppermute | solution.py:36
  84.3 352.7 %reduce-scatter.5.cloned.1.call-start = ((), (), s32[]{:S(2)}) async-start(), calls=%async_computation.3 | async-start | bytes 9175040 | tf_op jit(solution)/shard_map/reduce_scatter | solution.py:117
  84.6 25.6 %collective-permute-start.6 = (bf16[128,2048]{1,0:T(8,128)(2,1)S(1)}, bf16[128,2048]{1,0:T(8,128)(2,1)S(1)}, u32[]{:S(2)}, u32[]{:S(2)}) collective-permute-start(bf16[128,2048]{1,0:T(8,128)(2,1)S(1)} %copy-done.1), channel_id=1, source_target_pairs={{0,16},{8,24},{16,0},{24,8},{1,17},{9,25},{17,1},{25,9},{2,18},{10... | collective-permute-start | bytes 1572872 | tf_op jit(solution)/shard_map/ppermute | solution.py:40
  87.3 46.6 %collective-permute-start.7 = (bf16[384,2048]{1,0:T(8,128)(2,1)}, bf16[384,2048]{1,0:T(8,128)(2,1)}, u32[]{:S(2)}, u32[]{:S(2)}) collective-permute-start(bf16[384,2048]{1,0:T(8,128)(2,1)} %fusion.12), channel_id=1, source_target_pairs={{0,16},{8,24},{16,0},{24,8},{1,17},{9,25},{17,1},{25,9},{2,18},{10... | collective-permute-start | bytes 4718600 | tf_op jit(solution)/shard_map/ppermute | solution.py:40
  123.3 2.0 collective-permute-start.11
  123.3 66.3 %collective-permute-start.8 = (bf16[640,2048]{1,0:T(8,128)(2,1)}, bf16[640,2048]{1,0:T(8,128)(2,1)S(1)}, u32[]{:S(2)}, u32[]{:S(2)}) collective-permute-start(bf16[640,2048]{1,0:T(8,128)(2,1)} %fusion.4), channel_id=1, source_target_pairs={{0,16},{8,24},{16,0},{24,8},{1,17},{9,25},{17,1},{25,9},{2,18},{10... | collective-permute-start | bytes 7864328 | tf_op jit(solution)/shard_map/ppermute | solution.py:40
  140.5 3.8 collective-permute-start.12
  196.4 12.5 %collective-permute-start.13 = (bf16[640,2048]{1,0:T(8,128)(2,1)}, bf16[640,2048]{1,0:T(8,128)(2,1)}, u32[]{:S(2)}, u32[]{:S(2)}) collective-permute-start(bf16[640,2048]{1,0:T(8,128)(2,1)} %get-tuple-element.29), channel_id=1, source_target_pairs={{0,8},{8,0},{16,24},{24,16},{1,9},{9,1},{17,25},{25,17},{2,10},{10... | collective-permute-start | bytes 7864328 | tf_op jit(solution)/shard_map/ppermute | solution.py:36
  196.4 48.8 %collective-permute-start.9 = (bf16[512,2048]{1,0:T(8,128)(2,1)}, bf16[512,2048]{1,0:T(8,128)(2,1)}, u32[]{:S(2)}, u32[]{:S(2)}) collective-permute-start(bf16[512,2048]{1,0:T(8,128)(2,1)} %fusion.8), channel_id=1, source_target_pairs={{0,16},{8,24},{16,0},{24,8},{1,17},{9,25},{17,1},{25,9},{2,18},{10... | collective-permute-start | bytes 6291464 | tf_op jit(solution)/shard_map/ppermute | solution.py:40
  198.1 67.7 %collective-permute-start.16 = (bf16[128,2048]{1,0:T(8,128)(2,1)S(1)}, bf16[128,2048]{1,0:T(8,128)(2,1)S(1)}, u32[]{:S(2)}, u32[]{:S(2)}) collective-permute-start(bf16[128,2048]{1,0:T(8,128)(2,1)S(1)} %get-tuple-element.33), channel_id=1, source_target_pairs={{0,16},{8,24},{16,0},{24,8},{1,17},{9,25},{17,1},{25,9},{2,18},{10... | collective-permute-start | bytes 1572872 | tf_op jit(solution)/shard_map/ppermute | solution.py:40
  198.4 53.1 %slice-start = ((s8[14680064]{0:T(1024)(128)(4,1)}), s8[4194304]{0:T(1024)(128)(4,1)S(1)}, s32[]{:S(2)}) async-start(s8[14680064]{0:T(1024)(128)(4,1)} %bitcast.65), calls=%async_computation.5 | async-start | bytes 8388608
  198.4 53.1 %slice-start.1 = ((s8[14680064]{0:T(1024)(128)(4,1)}), s8[4194304]{0:T(1024)(128)(4,1)S(1)}, s32[]{:S(2)}) async-start(s8[14680064]{0:T(1024)(128)(4,1)} %bitcast.65), calls=%async_computation.6 | async-start | bytes 8388608
  207.1 139.2 %collective-permute-start.20 = (bf16[640,2048]{1,0:T(8,128)(2,1)}, bf16[640,2048]{1,0:T(8,128)(2,1)}, u32[]{:S(2)}, u32[]{:S(2)}) collective-permute-start(bf16[640,2048]{1,0:T(8,128)(2,1)} %get-tuple-element.29), channel_id=1, source_target_pairs={{0,16},{8,24},{16,0},{24,8},{1,17},{9,25},{17,1},{25,9},{2,18},{10... | collective-permute-start | bytes 7864328 | tf_op jit(solution)/shard_map/ppermute | solution.py:40
  208.8 42.7 %slice-start.2 = ((s8[14680064]{0:T(1024)(128)(4,1)}), s8[4194304]{0:T(1024)(128)(4,1)S(1)}, s32[]{:S(2)}) async-start(s8[14680064]{0:T(1024)(128)(4,1)} %bitcast.65), calls=%async_computation.7 | async-start | bytes 8388608
  251.5 95.3 %collective-permute-start.14 = (bf16[512,2048]{1,0:T(8,128)(2,1)}, bf16[512,2048]{1,0:T(8,128)(2,1)}, u32[]{:S(2)}, u32[]{:S(2)}) collective-permute-start(bf16[512,2048]{1,0:T(8,128)(2,1)} %get-tuple-element.27), channel_id=1, source_target_pairs={{0,8},{8,0},{16,24},{24,16},{1,9},{9,1},{17,25},{25,17},{2,10},{10... | collective-permute-start | bytes 6291464 | tf_op jit(solution)/shard_map/ppermute | solution.py:36
  256.8 89.5 %collective-permute-start.18 = (bf16[384,2048]{1,0:T(8,128)(2,1)}, bf16[384,2048]{1,0:T(8,128)(2,1)}, u32[]{:S(2)}, u32[]{:S(2)}) collective-permute-start(bf16[384,2048]{1,0:T(8,128)(2,1)} %get-tuple-element.31), channel_id=1, source_target_pairs={{0,16},{8,24},{16,0},{24,8},{1,17},{9,25},{17,1},{25,9},{2,18},{10... | collective-permute-start | bytes 4718600 | tf_op jit(solution)/shard_map/ppermute | solution.py:40
  258.6 145.8 %collective-permute-start.22 = (bf16[512,2048]{1,0:T(8,128)(2,1)}, bf16[512,2048]{1,0:T(8,128)(2,1)}, u32[]{:S(2)}, u32[]{:S(2)}) collective-permute-start(bf16[512,2048]{1,0:T(8,128)(2,1)} %get-tuple-element.27), channel_id=1, source_target_pairs={{0,16},{8,24},{16,0},{24,8},{1,17},{9,25},{17,1},{25,9},{2,18},{10... | collective-permute-start | bytes 6291464 | tf_op jit(solution)/shard_map/ppermute | solution.py:40
  265.9 136.1 %collective-permute-start.10 = (bf16[128,2048]{1,0:T(8,128)(2,1)S(1)}, bf16[128,2048]{1,0:T(8,128)(2,1)S(1)}, u32[]{:S(2)}, u32[]{:S(2)}) collective-permute-start(bf16[128,2048]{1,0:T(8,128)(2,1)S(1)} %copy-done), channel_id=1, source_target_pairs={{0,16},{8,24},{16,0},{24,8},{1,17},{9,25},{17,1},{25,9},{2,18},{10... | collective-permute-start | bytes 1572872 | tf_op jit(solution)/shard_map/ppermute | solution.py:40
  346.3 74.1 %collective-permute-start.17 = (bf16[128,2048]{1,0:T(8,128)(2,1)S(1)}, bf16[128,2048]{1,0:T(8,128)(2,1)S(1)}, u32[]{:S(2)}, u32[]{:S(2)}) collective-permute-start(bf16[128,2048]{1,0:T(8,128)(2,1)S(1)} %collective-permute-done.16), channel_id=1, source_target_pairs={{0,8},{8,0},{16,24},{24,16},{1,9},{9,1},{17,25},{25,17},{2,10},{10... | collective-permute-start | bytes 1572872 | tf_op jit(solution)/shard_map/ppermute | solution.py:36
  346.3 77.7 %collective-permute-start.19 = (bf16[384,2048]{1,0:T(8,128)(2,1)}, bf16[384,2048]{1,0:T(8,128)(2,1)S(1)}, u32[]{:S(2)}, u32[]{:S(2)}) collective-permute-start(bf16[384,2048]{1,0:T(8,128)(2,1)} %collective-permute-done.18), channel_id=1, source_target_pairs={{0,8},{8,0},{16,24},{24,16},{1,9},{9,1},{17,25},{25,17},{2,10},{10... | collective-permute-start | bytes 4718600 | tf_op jit(solution)/shard_map/ppermute | solution.py:36
  346.8 82.0 %collective-permute-start.21 = (bf16[640,2048]{1,0:T(8,128)(2,1)}, bf16[640,2048]{1,0:T(8,128)(2,1)S(1)}, u32[]{:S(2)}, u32[]{:S(2)}) collective-permute-start(bf16[640,2048]{1,0:T(8,128)(2,1)} %collective-permute-done.20), channel_id=1, source_target_pairs={{0,8},{8,0},{16,24},{24,16},{1,9},{9,1},{17,25},{25,17},{2,10},{10... | collective-permute-start | bytes 7864328 | tf_op jit(solution)/shard_map/ppermute | solution.py:36
  404.4 4.3 collective-permute-start.15
  404.4 14.3 %collective-permute-start.24 = (bf16[128,2048]{1,0:T(8,128)(2,1)S(1)}, bf16[128,2048]{1,0:T(8,128)(2,1)S(1)}, u32[]{:S(2)}, u32[]{:S(2)}) collective-permute-start(bf16[128,2048]{1,0:T(8,128)(2,1)S(1)} %get-tuple-element.25), channel_id=1, source_target_pairs={{0,16},{8,24},{16,0},{24,8},{1,17},{9,25},{17,1},{25,9},{2,18},{10... | collective-permute-start | bytes 1572872 | tf_op jit(solution)/shard_map/ppermute | solution.py:40
  408.7 25.0 %collective-permute-start.23 = (bf16[512,2048]{1,0:T(8,128)(2,1)}, bf16[512,2048]{1,0:T(8,128)(2,1)S(1)}, u32[]{:S(2)}, u32[]{:S(2)}) collective-permute-start(bf16[512,2048]{1,0:T(8,128)(2,1)} %collective-permute-done.22), channel_id=1, source_target_pairs={{0,8},{8,0},{16,24},{24,16},{1,9},{9,1},{17,25},{25,17},{2,10},{10... | collective-permute-start | bytes 6291464 | tf_op jit(solution)/shard_map/ppermute | solution.py:36
  418.8 17.4 %collective-permute-start.25 = (bf16[128,2048]{1,0:T(8,128)(2,1)S(1)}, bf16[128,2048]{1,0:T(8,128)(2,1)S(1)}, u32[]{:S(2)}, u32[]{:S(2)}) collective-permute-start(bf16[128,2048]{1,0:T(8,128)(2,1)S(1)} %collective-permute-done.24), channel_id=1, source_target_pairs={{0,8},{8,0},{16,24},{24,16},{1,9},{9,1},{17,25},{25,17},{2,10},{10... | collective-permute-start | bytes 1572872 | tf_op jit(solution)/shard_map/ppermute | solution.py:36
  (3 other events, 72.5 us)
Sparse Core Ops, SparseCore 0:
  47.9 35.4 all-gather.2
  86.3 32.5 reduce-scatter.2
  121.7 127.7 reduce-scatter.4
